TPU v7x, 32 devices: a whole 2x2x4 slice. The times are simulated.
32 devices in a mesh: dp: 16 (over z, y, x), rep: 2 (over core).
Axes of the slice: x: 2, y: 2, z: 4, core: 2. Of those that a mesh axis runs over, the one named last changes fastest.
Arguments:
- row_grads: float32 [16384, 512], P(('dp', 'rep')), may hold values from -2500 to 2500
- token_owner: int32 [16384, 1], P(('dp', 'rep')), may hold values from 0 to 15; in each aligned block of 512 rows (0 to 511, 512 to 1023, ...) at most 64 rows name the same one
- token_row: int32 [16384], P(('dp', 'rep')), may hold values from 0 to 8191
- table: float32 [131072, 512], P('dp'), may hold values from -6 to 6
- moment: float32 [131072, 512], P('dp'), may hold values from -3 to 3
- second: float32 [131072, 512], P('dp'), may hold values from 0.05 to 2
Outputs:
- new_table: float32 [131072, 512], P('dp')
- new_moment: float32 [131072, 512], P('dp')
- new_second: float32 [131072, 512], P('dp')
Inputs may be any that keep to these rules, and one draw needn't show every extreme that they name: `token_owner`: among the rows of one device at most 64 name one owner; in every draw some owner is named by exactly 64 rows of some device.
All inputs are finite; a program needn't handle non-finite values.
Results may differ from a plain program's by a relative error of at most 0.00007.
Values sent between devices are 32-bit elements; how exact they have to be, the bound alone decides.
A program may use at most 192 MiB of HBM per device.

v0:
```python
import jax
import jax.numpy as jnp
from jax import lax
from jax.sharding import PartitionSpec as P

VOCAB = 131072
ADAM_STEP = 100
LW = 512


def accumulate(row_ids, sent_rows, row_start, row_count):
    local_ids = row_ids - row_start
    feature_cols = sent_rows.shape[1]
    inside = (local_ids >= 0) & (local_ids < row_count)
    slot_index = jnp.where(inside, local_ids, row_count)
    return (
        jnp.zeros((row_count, feature_cols), jnp.float32).at[slot_index].add(sent_rows, mode="drop")
    )


def adamw(table_rows, moment_rows, second_rows, dense_grad, scaling):
    clipped = scaling * dense_grad
    new_moment = 0.9 * moment_rows + 0.1 * clipped
    new_second = 0.999 * second_rows + 0.001 * clipped * clipped
    first_fix = 1.0 - 0.9**ADAM_STEP
    second_fix = 1.0 - 0.999**ADAM_STEP
    update = new_moment / first_fix / (jnp.sqrt(new_second / second_fix) + 1e-08)
    new_table = table_rows - 0.01 * (update + 0.01 * table_rows)
    return (new_table, new_moment, new_second)


def clip_factor(total):
    limit = 0.5 * jnp.sqrt(jnp.float32(VOCAB * LW))
    return jnp.minimum(jnp.float32(1.0), limit / (jnp.sqrt(total) + 1e-06))


def local(row_grads, token_owner, token_row, table, moment, second):
    owners = lax.axis_size("dp")
    tokens_here = row_grads.shape[0]
    feature_cols = row_grads.shape[1]
    rows_owned = table.shape[0]
    capacity = 2 * tokens_here // owners
    owner_ids = token_owner[:, 0]
    owner_hits = (owner_ids[:, None] == jnp.arange(owners, dtype=jnp.int32)[None, :]).astype(
        jnp.int32
    )
    earlier = jnp.cumsum(owner_hits, axis=0) - owner_hits
    position = jnp.sum(earlier * owner_hits, axis=1)
    destination = owner_ids * capacity + position
    send_rows = (
        jnp.zeros((owners * capacity, feature_cols), jnp.float32).at[destination].set(row_grads)
    )
    send_ids = jnp.zeros((owners * capacity,), jnp.int32).at[destination].set(token_row)
    received, received_ids = (
        lax.all_to_all(
            send_rows.reshape(owners, capacity, feature_cols),
            "dp",
            split_axis=0,
            concat_axis=0,
            tiled=True,
        ),
        lax.all_to_all(
            send_ids.reshape(owners, capacity), "dp", split_axis=0, concat_axis=0, tiled=True
        ),
    )
    flat_rows = received.reshape(owners * capacity, feature_cols)
    flat_ids = received_ids.reshape(owners * capacity)
    dense = lax.psum(accumulate(flat_ids, flat_rows, 0, rows_owned), "rep")
    total = lax.psum(jnp.sum(dense * dense), "dp")
    scaling = clip_factor(total)
    new_table, new_moment, new_second = adamw(table, moment, second, dense, scaling)
    return (new_table, new_moment, new_second)


def solution(mesh):
    return jax.shard_map(
        local,
        mesh=mesh,
        in_specs=(
            P(("dp", "rep"), None),
            P(("dp", "rep"), None),
            P(("dp", "rep")),
            P("dp", None),
            P("dp", None),
            P("dp", None),
        ),
        out_specs=(P("dp", None), P("dp", None), P("dp", None)),
        check_vma=False,
    )
```

profile of v0, /device:TPU:0, one launch (start us, length us, event | category | flops | bytes accessed | tf_op | source)
XLA Modules:
  0.0 257.8 jit_solution(1508270315383922822)
XLA Ops:
  7.2 0.7 fusion.8
  7.9 1.1 reduce-window.6
  9.0 0.2 slice_reduce_fusion
  9.2 0.8 fusion.7
  10.0 0.7 compare_select_fusion.1
  10.7 2.6 %scatter_custom_fusion = s32[1024]{0:T(1024)S(1)} fusion(s32[512]{0:T(512)S(1)} %bitcast.33, s32[512]{0:T(512)} %param.8, s32[]{:T(128)} %constant.19.clone.1), kind=kCustom, calls=%fused_computation.24 | custom fusion | bytes 4608 | tf_op jit(solution)/shard_map/scatter | solution.py:53
  13.3 0.7 all_to_all.9
  14.0 8.3 %all-to-all-start = ((s32[16,1,64]{2,1,0:T(1,128)}), s32[16,1,64]{2,1,0:T(1,128)S(1)}, u32[]{:S(2)}, u32[]{:S(2)}) async-start(s32[16,1,64]{2,1,0:T(1,128)} %all_to_all.9), calls=%async_computation | async-start | bytes 16384 | tf_op jit(solution)/shard_map/all_to_all | solution.py:62
  22.3 4.3 %scatter_custom_fusion.1 = f32[1024,512]{1,0:T(8,128)} fusion(s32[512]{0:T(512)S(1)} %bitcast.34, f32[512,512]{1,0:T(8,128)} %param.6, f32[]{:T(128)} %constant.18.clone.1), kind=kCustom, calls=%fused_computation.10 | custom fusion | bytes 2097664 | tf_op jit(solution)/shard_map/scatter | solution.py:51
  26.7 2.9 %all-to-all-done = s32[16,1,64]{2,1,0:T(1,128)S(1)} async-done(((s32[16,1,64]{2,1,0:T(1,128)}), s32[16,1,64]{2,1,0:T(1,128)S(1)}, u32[]{:S(2)}, u32[]{:S(2)}) %all-to-all-start) | async-done | bytes 4128 | tf_op jit(solution)/shard_map/all_to_all | solution.py:62
  29.6 4.0 %all-to-all-start.1 = ((f32[16,64,512]{2,1,0:T(8,128)}), f32[16,64,512]{2,1,0:T(8,128)S(1)}, u32[]{:S(2)}, u32[]{:S(2)}) async-start(f32[16,64,512]{2,1,0:T(8,128)} %bitcast.6), calls=%async_computation.1 | async-start | bytes 4194304 | tf_op jit(solution)/shard_map/all_to_all | solution.py:55
  33.6 0.0 all-reduce.2.cloned.1.call-start
  33.6 0.5 broadcast.92
  34.1 0.7 reduce.5
  34.8 0.1 reshape.78
  34.9 41.4 %all-to-all-done.1 = f32[16,64,512]{2,1,0:T(8,128)S(1)} async-done(((f32[16,64,512]{2,1,0:T(8,128)}), f32[16,64,512]{2,1,0:T(8,128)S(1)}, u32[]{:S(2)}, u32[]{:S(2)}) %all-to-all-start.1) | async-done | bytes 2097184 | tf_op jit(solution)/shard_map/all_to_all | solution.py:55
  76.3 14.1 %scatter_custom_fusion.2 = f32[8192,512]{1,0:T(8,128)} fusion(s32[1024]{0:T(1024)S(1)} %bitcast.32, f32[1024,512]{1,0:T(8,128)S(1)} %bitcast.28, f32[]{:T(128)} %constant.18.clone.1), kind=kCustom, calls=%fused_computation.8 | custom fusion | flops 524288 | bytes 16777220 | tf_op jit(solution)/shard_map/scatter-add | solution.py:17
  90.4 0.0 all-reduce.2.cloned.1.call-update
  90.4 65.4 %all-reduce.2.cloned.1.call-done = f32[8192,512]{1,0:T(8,128)} async-done(((f32[8192,512]{1,0:T(8,128)}), f32[8192,512]{1,0:T(8,128)}) %all-reduce.2.cloned.1.call-update) | async-done | bytes 16777232 | tf_op jit(solution)/shard_map/psum | solution.py:68
  155.8 10.7 %multiply_reduce_fusion = f32[]{:T(128)} fusion(f32[8192,512]{1,0:T(8,128)} %all-reduce.2.cloned.1.call-done), kind=kLoop, calls=%fused_computation.7 | loop fusion | flops 8388607 | bytes 16777220 | tf_op jit(solution)/shard_map/reduce_sum | solution.py:69
  166.5 42.8 %psum.15 = f32[]{:T(128)} all-reduce(f32[]{:T(128)} %multiply_reduce_fusion), channel_id=1, replica_groups=mesh['dp'=16,'rep'=2] {'dp'}, use_global_device_ids=true, to_apply=%region_8.9 | all-reduce | flops 1 | bytes 8 | tf_op jit(solution)/shard_map/psum | solution.py:69
  210.0 40.9 %multiply_subtract_fusion = (f32[8192,512]{1,0:T(8,128)}, f32[8192,512]{1,0:T(8,128)}, f32[8192,512]{1,0:T(8,128)}) fusion(f32[8192,512]{1,0:T(8,128)} %param.9, f32[8192,512]{1,0:T(8,128)} %all-reduce.2.cloned.1.call-done, f32[]{:T(128)S(6)} %min_shard_map.3, f32[8192,512]{1,0:T(8,128)} %param.10, f32[8192,512]{1,0:T(8,128)} %param.11), kind=kLoop, calls=%fused_computation.5 | loop fusion | flops 67108864 | bytes 117440512 | tf_op jit(solution)/shard_map/sub | solution.py:28
  (3 shorter events, 0.1 us)
Async XLA Ops:
  14.0 15.6 %all-to-all-start = ((s32[16,1,64]{2,1,0:T(1,128)}), s32[16,1,64]{2,1,0:T(1,128)S(1)}, u32[]{:S(2)}, u32[]{:S(2)}) async-start(s32[16,1,64]{2,1,0:T(1,128)} %all_to_all.9), calls=%async_computation | async-start | bytes 16384 | tf_op jit(solution)/shard_map/all_to_all | solution.py:62
  29.6 46.7 %all-to-all-start.1 = ((f32[16,64,512]{2,1,0:T(8,128)}), f32[16,64,512]{2,1,0:T(8,128)S(1)}, u32[]{:S(2)}, u32[]{:S(2)}) async-start(f32[16,64,512]{2,1,0:T(8,128)} %bitcast.6), calls=%async_computation.1 | async-start | bytes 4194304 | tf_op jit(solution)/shard_map/all_to_all | solution.py:55
  33.6 122.2 %all-reduce.2.cloned.1.call-start = ((), (), s32[]{:S(2)}) async-start(), calls=%async_computation.2 | async-start | bytes 33554432 | tf_op jit(solution)/shard_map/psum | solution.py:68
Sparse Core Ops, SparseCore 0:
  90.6 65.2 all-reduce.1
where the time goes:
time: 258 us
  waiting for transfers between devices  110 us (43%)
  other arithmetic  69.7 us (27%)
  blocking collectives  42.8 us (17%)
  between operations  14.8 us (6%)
  starting transfers between devices  12.4 us (5%)
  local copies, waits for them, and re-layouts  8.41 us (3%)
    psum x1, waiting for transfers between devices, local(): dense = lax.psum(accumulate(flat_ids, flat_rows, 0, rows_owned), 'rep')  65.4 us
    psum x1, blocking collectives, local(): total = lax.psum(jnp.sum(dense * dense), 'dp')  42.8 us
    all_to_all x1, waiting for transfers between devices, local(): lax.all_to_all(send_rows.reshape(owners, capacity, feature_cols), 'dp', s...  41.4 us
    sub x1, other arithmetic, adamw(): new_table = table_rows - 0.01 * (update + 0.01 * table_rows)  40.9 us
    scatter-add x1, other arithmetic, accumulate(): jnp.zeros((row_count, feature_cols), jnp.float32).at[slot_index]  14.1 us
    reduce_sum x1, other arithmetic, local(): total = lax.psum(jnp.sum(dense * dense), 'dp')  10.7 us
    all_to_all x1, starting transfers between devices, local(): lax.all_to_all(send_ids.reshape(owners, capacity), 'dp', split_axis=0, co...  8.34 us
  transfers between devices with their start and end apart: 3, of which 3 were waited for; matrix products, arithmetic and copies ran while one was open for 2% of the time, Pallas kernels for 0%

commit v1 on v0

v1 whole, which is shorter than its diff:
```python
import functools

import jax
import jax.numpy as jnp
from jax import lax
from jax.experimental import pallas as pl
from jax.experimental.pallas import tpu as pltpu
from jax.sharding import PartitionSpec as P

ADAM_STEP = 100
SMEM = pl.BlockSpec(memory_space=pltpu.SMEM)
VMEM = pl.BlockSpec(memory_space=pltpu.VMEM)
ANY = pl.BlockSpec(memory_space=pl.ANY)
MIB = 1 << 20


def pack_kernel(owners, capacity, owner_ref, row_ref, grads_ref, rows_out, ids_out):
    def clear(o, carry):
        ids_out[o, capacity] = 0
        return carry

    lax.fori_loop(0, owners, clear, 0)

    def token(t, carry):
        o = owner_ref[t]
        p = ids_out[o, capacity]
        ids_out[o, capacity] = p + 1
        ids_out[o, p] = row_ref[t]
        rows_out[pl.ds(o * capacity + p, 1), :] = grads_ref[pl.ds(t, 1), :]
        return carry

    lax.fori_loop(0, owner_ref.shape[0], token, 0, unroll=4)


def pack(row_grads, owner_ids, token_row, owners, capacity):
    tokens, cols = row_grads.shape
    return pl.pallas_call(
        functools.partial(pack_kernel, owners, capacity),
        out_shape=(
            jax.ShapeDtypeStruct((owners * capacity, cols), jnp.float32),
            jax.ShapeDtypeStruct((owners, capacity + 1), jnp.int32),
        ),
        in_specs=[SMEM, SMEM, VMEM],
        out_specs=(VMEM, SMEM),
        compiler_params=pltpu.CompilerParams(vmem_limit_bytes=6 * MIB),
    )(owner_ids, token_row, row_grads)


def sum_kernel(owners, capacity, rep_ref, own_ids, other_ids, own_ref, other_ref, out_ref, total_ref, dense_ref, sem):
    rows, cols = out_ref.shape
    step = 64

    def clear(i, carry):
        dense_ref[pl.ds(pl.multiple_of(i * step, step), step), :] = jnp.zeros((step, cols), jnp.float32)
        return carry

    lax.fori_loop(0, rows // step, clear, 0)

    def add(ids, ref):
        def source(s, carry):
            count = ids[s, capacity]

            def pair(j, inner):
                i = 2 * j
                r0 = ids[s, i]
                r1 = jnp.where(i + 1 < count, ids[s, i + 1], rows)
                d0 = dense_ref[pl.ds(r0, 1), :]
                d1 = dense_ref[pl.ds(r1, 1), :]
                n0 = d0 + ref[pl.ds(s * capacity + i, 1), :]
                n1 = jnp.where(r0 == r1, n0, d1) + ref[pl.ds(s * capacity + i + 1, 1), :]
                dense_ref[pl.ds(r0, 1), :] = n0
                dense_ref[pl.ds(r1, 1), :] = n1
                return inner

            return lax.fori_loop(0, (count + 1) // 2, pair, carry)

        lax.fori_loop(0, owners, source, 0)

    for core in range(2):
        mine = rep_ref[0] == core

        @pl.when(mine)
        def _():
            add(own_ids, own_ref)

        @pl.when(jnp.logical_not(mine))
        def _():
            add(other_ids, other_ref)

    copy = pltpu.make_async_copy(dense_ref.at[pl.ds(0, rows)], out_ref, sem)
    copy.start()

    def square(i, acc):
        block = dense_ref[pl.ds(pl.multiple_of(i * step, step), step), :]
        return acc + jnp.sum((block * block).reshape(step // 8, 8, cols), axis=0)

    acc = lax.fori_loop(0, rows // step, square, jnp.zeros((8, cols), jnp.float32))
    total_ref[0, 0] = jnp.sum(acc)
    copy.wait()


def accumulate(rep, own_ids, other_ids, own, other, rows):
    owners, width = own_ids.shape
    cols = own.shape[1]
    return pl.pallas_call(
        functools.partial(sum_kernel, owners, width - 1),
        out_shape=(
            jax.ShapeDtypeStruct((rows, cols), jnp.float32),
            jax.ShapeDtypeStruct((1, 1), jnp.float32),
        ),
        in_specs=[SMEM, SMEM, SMEM, VMEM, VMEM],
        out_specs=(ANY, SMEM),
        scratch_shapes=[pltpu.VMEM((rows + 8, cols), jnp.float32), pltpu.SemaphoreType.DMA],
        compiler_params=pltpu.CompilerParams(vmem_limit_bytes=58 * MIB),
    )(rep, own_ids, other_ids, own, other)


def adamw(clip, dense, moment, second, table):
    g = clip * dense
    new_moment = 0.9 * moment + 0.1 * g
    new_second = 0.999 * second + 0.001 * g * g
    first_fix = 1.0 - 0.9**ADAM_STEP
    second_fix = 1.0 - 0.999**ADAM_STEP
    update = new_moment / first_fix / (jnp.sqrt(new_second / second_fix) + 1e-08)
    return (table - 0.01 * (update + 0.01 * table), new_moment, new_second)


def local(row_grads, token_owner, token_row, table, moment, second):
    owners = lax.axis_size("dp")
    tokens, cols = row_grads.shape
    capacity = 2 * tokens // owners
    send_rows, send_ids = pack(row_grads, token_owner.reshape(tokens), token_row, owners, capacity)
    got = lax.all_to_all(
        send_rows.reshape(owners, capacity, cols), "dp", split_axis=0, concat_axis=0, tiled=True
    ).reshape(owners * capacity, cols)
    got_ids = lax.all_to_all(send_ids, "dp", split_axis=0, concat_axis=0, tiled=True)
    swap = [(0, 1), (1, 0)]
    other_ids = lax.ppermute(got_ids, "rep", swap)
    other = lax.ppermute(got, "rep", swap)
    rep = lax.axis_index("rep").reshape(1).astype(jnp.int32)
    dense, total = accumulate(rep, got_ids, other_ids, got, other, table.shape[0])
    totals = lax.all_to_all(
        jnp.broadcast_to(total.reshape(1, 1, 1), (owners, 1, 128)), "dp", split_axis=0, concat_axis=0, tiled=True
    )
    total = jnp.sum(totals[:, 0, :1], axis=0, keepdims=True)
    entries = owners * table.shape[0] * cols
    limit = 0.5 * jnp.sqrt(jnp.float32(entries))
    clip = jnp.minimum(jnp.float32(1.0), limit / (jnp.sqrt(total) + 1e-06))
    return adamw(clip, dense, moment, second, table)


def solution(mesh):
    return jax.shard_map(
        local,
        mesh=mesh,
        in_specs=(
            P(("dp", "rep"), None),
            P(("dp", "rep"), None),
            P(("dp", "rep")),
            P("dp", None),
            P("dp", None),
            P("dp", None),
        ),
        out_specs=(P("dp", None), P("dp", None), P("dp", None)),
        check_vma=False,
    )
```

time: 258 us -> 158 us (0.61)
  waiting for transfers between devices: 110 us -> 1.17 us
  blocking collectives: 42.8 us -> 86.5 us
  other arithmetic: 69.7 us -> 41.5 us
  Pallas kernels: 0 us -> 23.6 us
  between operations: 14.8 us -> 1.42 us
  starting transfers between devices: 12.4 us -> 0.01 us
  local copies, waits for them, and re-layouts: 8.41 us -> 3.78 us
    all_to_all x0 -> x3, blocking collectives: none -> 86.5 us  [the longest x1 56.9 us: local(): lax.all_to_all(send_rows.reshape(owners, capacity, cols), 'dp', split_axi...]
    psum x1 -> x0, waiting for transfers between devices: 65.4 us -> none  [local(): dense = lax.psum(accumulate(flat_ids, flat_rows, 0, rows_owned), 'rep')]
    all_to_all x2 -> x0, waiting for transfers between devices: 44.3 us -> none  [the longest x1 41.4 us: local(): lax.all_to_all(send_rows.reshape(owners, capacity, feature_cols), 'dp', s...]
    psum x1 -> x0, blocking collectives: 42.8 us -> none  [local(): total = lax.psum(jnp.sum(dense * dense), 'dp')]
    pallas_call x0 -> x2, Pallas kernels: none -> 23.6 us  [the longest x1 17.6 us: accumulate(): pl.pallas_call(functools.partial(sum_kernel, owners, width - 1), out_shap...]
    scatter-add x1 -> x0, other arithmetic: 14.1 us -> none  [accumulate(): jnp.zeros((row_count, feature_cols), jnp.float32).at[slot_index]]
    all_to_all x2 -> x0, starting transfers between devices: 12.3 us -> none  [the longest x1 8.34 us: local(): lax.all_to_all(send_ids.reshape(owners, capacity), 'dp', split_axis=0, co...]
    reduce_sum x2 -> x1, other arithmetic: 11.5 us -> 0.62 us  [local(): total = jnp.sum(totals[:, 0, :1], axis=0, keepdims=True)]
  transfers between devices with their start and end apart: 3 -> 2, of which waited for: 3 -> 1; matrix products, arithmetic and copies ran while one was open for 2% -> 0% of each run, Pallas kernels for 0% -> 0%
where the time goes in v1:
time: 158 us
  blocking collectives  86.5 us (55%)
  other arithmetic  41.5 us (26%)
  Pallas kernels  23.6 us (15%)
  local copies, waits for them, and re-layouts  3.78 us (2%)
    all_to_all x1, blocking collectives, local(): lax.all_to_all(send_rows.reshape(owners, capacity, cols), 'dp', split_axi...  56.9 us
    sub x1, other arithmetic, adamw(): return (table - 0.01 * (update + 0.01 * table), new_moment, new_second)  40.9 us
    all_to_all x1, blocking collectives, local(): lax.all_to_all(jnp.broadcast_to(total.reshape(1, 1, 1), (owners, 1, 128))...  18.5 us
    pallas_call x1, Pallas kernels, accumulate(): pl.pallas_call(functools.partial(sum_kernel, owners, width - 1), out_shap...  17.6 us
    all_to_all x1, blocking collectives, local(): lax.all_to_all(send_ids, 'dp', split_axis=0, concat_axis=0, tiled=True)  11 us
    pallas_call x1, Pallas kernels, pack(): pl.pallas_call(functools.partial(pack_kernel, owners, capacity), out_shap...  5.99 us
    unnamed x12, local copies, waits for them, and re-layouts  3.16 us
  transfers between devices with their start and end apart: 2, of which 1 were waited for; matrix products, arithmetic and copies ran while one was open for 0% of the time, Pallas kernels for 0%

profile of v1, /device:TPU:0, one launch (start us, length us, event | category | flops | bytes accessed | tf_op | source)
XLA Modules:
  0.0 158.0 jit_solution(8381882953273730404)
XLA Ops:
  0.6 0.0 copy-start
  0.6 1.2 copy-done
  1.9 0.0 copy-start.1
  1.9 0.7 copy-done.1
  2.5 0.0 copy-start.2
  2.5 0.7 copy-done.2
  3.2 6.0 %shard_map.85 = (f32[1024,512]{1,0:T(8,128)S(1)}, s32[16,65]{1,0:T(8,128)S(1)}) custom-call(s32[512]{0:T(512)S(1)} %bitcast.11, s32[512]{0:T(512)S(1)} %copy-done.2, f32[512,512]{1,0:T(8,128)S(1)} %copy-done), custom_call_target="tpu_custom_call" | custom-call | tf_op jit(solution)/shard_map/pallas_call | solution.py:37
  9.2 56.9 %all_to_all.21 = f32[16,64,512]{2,1,0:T(8,128)S(1)} all-to-all(f32[16,64,512]{2,1,0:T(8,128)S(1)} %bitcast.9), channel_id=1, replica_groups=mesh['dp'=16,'rep'=2] {'dp'}, dimensions={0} | all-to-all | bytes 4194304 | tf_op jit(solution)/shard_map/all_to_all | solution.py:133
  66.1 0.0 copy-start.3
  66.2 0.0 collective-permute-start.1
  66.2 11.0 %all_to_all.22 = s32[16,1,65]{2,1,0:T(1,128)S(1)} all-to-all(s32[16,1,65]{2,1,0:T(1,128)S(1)} %bitcast.10), channel_id=1, replica_groups=mesh['dp'=16,'rep'=2] {'dp'}, dimensions={0} | all-to-all | bytes 8320 | tf_op jit(solution)/shard_map/all_to_all | solution.py:136
  77.2 0.0 copy-start.4
  77.2 0.0 collective-permute-start
  77.2 1.2 collective-permute-done.other_ids
  78.4 0.0 copy-start.5
  78.4 0.0 collective-permute-done.1.other_ref
  78.4 0.0 copy-done.3
  78.4 0.0 copy-done.4
  78.4 0.6 copy-done.5
  79.0 17.6 %shard_map.86 = (f32[8192,512]{1,0:T(8,128)}, f32[1,1]{1,0:T(1,128)}) custom-call(s32[1]{0:T(128)} %bitcast.rep_ref, s32[16,65]{1,0:T(8,128)} %bitcast.15, s32[16,65]{1,0:T(8,128)} %copy-done.5, f32[1024,512]{1,0:T(8,128)} %bitcast.13, f32[1024,512]{1,0:T(8,128)} %collective-permute-done.1.other_ref), custom_call_target="tpu_custom_call" | custom-call | tf_op jit(solution)/shard_map/pallas_call | solution.py:105
  96.6 0.6 broadcast_in_dim.9
  97.2 18.5 %all_to_all.23 = f32[16,1,128]{2,1,0:T(1,128)S(1)} all-to-all(f32[16,1,128]{2,1,0:T(1,128)S(1)} %broadcast_in_dim.9), channel_id=1, replica_groups=mesh['dp'=16,'rep'=2] {'dp'}, dimensions={0} | all-to-all | bytes 16384 | tf_op jit(solution)/shard_map/all_to_all | solution.py:142
  115.7 0.6 slice_reduce_fusion
  117.1 40.9 %multiply_subtract_fusion = (f32[8192,512]{1,0:T(8,128)}, f32[8192,512]{1,0:T(8,128)}, f32[8192,512]{1,0:T(8,128)}) fusion(f32[8192,512]{1,0:T(8,128)} %param.9, f32[8192,512]{1,0:T(8,128)} %get-tuple-element.10, f32[]{:T(128)S(6)} %min.4, f32[8192,512]{1,0:T(8,128)} %param.10, f32[8192,512]{1,0:T(8,128)} %param.11), kind=kLoop, calls=%fused_computation.2 | loop fusion | flops 67108864 | bytes 117440512 | tf_op jit(solution)/shard_map/sub | solution.py:125
Async XLA Ops:
  0.6 1.2 copy-start
  1.9 0.7 copy-start.1
  2.5 0.7 copy-start.2
  66.1 12.2 %copy-start.3 = (f32[16,64,512]{2,1,0:T(8,128)}, f32[16,64,512]{2,1,0:T(8,128)S(1)}, u32[]{:S(2)}) copy-start(f32[16,64,512]{2,1,0:T(8,128)S(1)} %all_to_all.21) | copy-start | bytes 6291460
  66.2 12.2 %collective-permute-start.1 = (f32[1024,512]{1,0:T(8,128)S(1)}, f32[1024,512]{1,0:T(8,128)}, u32[]{:S(2)}, u32[]{:S(2)}) collective-permute-start(f32[1024,512]{1,0:T(8,128)S(1)} %bitcast.12), channel_id=1, source_target_pairs={{0,1},{1,0},{2,3},{3,2},{4,5},{5,4},{6,7},{7,6},{8,9},{9,8},{10,11... | collective-permute-start | bytes 6291464 | tf_op jit(solution)/shard_map/ppermute | solution.py:139
  77.2 1.2 copy-start.4
  77.2 1.2 collective-permute-start
  78.4 0.6 copy-start.5
